TPU v7x, 256 devices: a whole 4x4x8 slice. The times are simulated.
256 devices in a mesh: dp: 128 (over z_hi, x, y, core), tensor: 2 (over z_lo).
Axes of the slice: x: 4, y: 4, z: 8 (z_hi: 4, z_lo: 2; z = z_hi * 2 + z_lo), core: 2. Of those that a mesh axis runs over, the one named last changes fastest.
Arguments:
- tokens: bfloat16 [16384, 1792], P('dp'), may hold values from -6 to 6
- targets: bfloat16 [16384, 1792], P('dp'), may hold values from -6 to 6
- live_mask: int32 [16384], P('dp'), may hold values from 0 to 1, as said below
- up_weight: bfloat16 [1792, 7168], P('dp', 'tensor'), may hold values from -0.125 to 0.125
- down_weight: bfloat16 [1792, 7168], P('dp', 'tensor'), may hold values from -0.0625 to 0.0625
- probe_rows: int32 [1792], replicated, may hold values from 0 to 16777215
- probe_cols: int32 [7168], P('tensor'), may hold values from 0 to 16777215
- moment: float32 [1792, 512], P('dp', 'tensor'), may hold values from 0.01 to 1
Outputs:
- hess_diag: float32 [1792, 512], P('dp', 'tensor')
- second_moment: float32 [1792, 512], P('dp', 'tensor')
- mean_loss: float32 [], replicated
Inputs may be any that keep to these rules, and one draw needn't show every extreme that they name: In every aligned block of 128 tokens the first token has live_mask 1.
All inputs are finite; a program needn't handle non-finite values.
Results may differ from a plain program's by a relative error of at most 0.0023.
Values may be sent and summed in bfloat16 or wider, within the bound.
No kernel may reach another device: no remote copies, remote signals or barrier semaphores. Data moves between devices by JAX's collectives and lax.ppermute only.
A program may use at most 128 MiB of HBM per device.

v0:
```python
import jax
import jax.numpy as jnp
from jax import lax
from jax.sharding import Mesh
from jax.sharding import PartitionSpec as P

BLOCK = 14
DP = ("dp_0", "dp_1", "dp_2", "dp_3")
DP_TENSOR = ("dp_0", "dp_1", "dp_2", "dp_3", "tensor")
gelu_coef = 0.7978845608028654
cubic_coef = 0.044715
beta_two = 0.999


def sent_to_all(shard, axis):
    copies = jnp.broadcast_to(shard, (lax.axis_size(axis), *shard.shape))
    return lax.all_to_all(copies, axis, split_axis=0, concat_axis=0, tiled=True)


def over_copies(shard, axis):
    everything = sent_to_all(shard, axis)
    return jnp.sum(everything, axis=0)


def together(arrays, axis):
    line, at, done = (jnp.concatenate([a.reshape(-1) for a in arrays]), 0, [])
    total = over_copies(line, axis)
    for a in arrays:
        done.append(total[at : at + a.size].reshape(a.shape))
        at += a.size
    return tuple(done)


def cut_along(shard, dim, count):
    before, after = (shard.shape[:dim], shard.shape[dim + 1 :])
    return jnp.moveaxis(shard.reshape(*before, count, -1, *after), dim, 0)


def sent_and_summed(shard, axis, dim):
    count = lax.axis_size(axis)
    tiles = lax.all_to_all(cut_along(shard, dim, count), axis, 0, 0, tiled=True)
    return jnp.sum(tiles, axis=0)


def sum_in_two_steps(shard, axes, dim):
    far, near = axes
    own = sent_and_summed(cut_along(shard, dim, lax.axis_size(far)), near, dim + 1)
    return jnp.sum(lax.all_to_all(own, far, 0, 0, tiled=True), axis=0)


def one_axis_at_a_time(shard, axes):
    for axis in axes:
        shard = lax.psum(shard, axis)
    return shard


def probe_signs(row_keys, col_keys):
    hashed = jnp.bitwise_xor(row_keys[:, None] * 747796405, col_keys[None, :])
    hashed = jnp.bitwise_xor(hashed, jnp.right_shift(hashed, 15) & 131071)
    hashed = hashed * 695872825
    hashed = jnp.bitwise_xor(hashed, jnp.right_shift(hashed, 13) & 524287)
    hashed = hashed * 739982445
    hashed = jnp.bitwise_xor(hashed, jnp.right_shift(hashed, 16) & 65535)
    parity = jnp.right_shift(hashed, 11) & 1
    return (2 * parity - 1).astype(jnp.bfloat16)


def gelu_parts(preact):
    tanh_arg = gelu_coef * (preact + cubic_coef * preact * preact * preact)
    tanh_val = jnp.tanh(tanh_arg)
    sech_sq = 1.0 - tanh_val * tanh_val
    arg_slope = gelu_coef * (1.0 + 3.0 * cubic_coef * preact * preact)
    arg_curve = gelu_coef * 6.0 * cubic_coef * preact
    gelu_value = 0.5 * preact * (1.0 + tanh_val)
    gelu_slope = 0.5 * (1.0 + tanh_val) + 0.5 * preact * sech_sq * arg_slope
    gelu_curve = sech_sq * (
        arg_slope - preact * tanh_val * arg_slope * arg_slope + 0.5 * preact * arg_curve
    )
    return (gelu_value, gelu_slope, gelu_curve)


def body(tokens, targets, live_mask, up_weight, down_weight, probe_rows, probe_cols, moment):
    tok_count = tokens.shape[0]
    ff_local = up_weight.shape[1]
    own_rows = up_weight.shape[0]
    tensor_count = lax.axis_size("tensor")
    live_rows = live_mask.astype(jnp.float32)
    local_count = jnp.sum(live_rows) * (1.0 / tensor_count)
    all_signs = probe_signs(probe_rows, probe_cols)
    columns = tokens
    sign_rows = all_signs
    joined = jnp.concatenate([lax.all_gather(up_weight, DP, axis=0, tiled=True), sign_rows], axis=1)
    both_pre = jnp.dot(columns, joined, preferred_element_type=jnp.float32)
    preact = both_pre[:, :ff_local]
    tangent = both_pre[:, ff_local:]
    full_down = lax.all_gather(down_weight, DP, axis=0, tiled=True)
    gelu_value, gelu_slope, gelu_curve = gelu_parts(preact)
    hidden = gelu_value.astype(jnp.bfloat16)
    hidden_dir = (gelu_slope * tangent).astype(jnp.bfloat16)
    stacked = jnp.concatenate([hidden, hidden_dir], axis=0)
    projected = jnp.einsum("tf,df->td", stacked, full_down, preferred_element_type=jnp.float32)
    outputs, out_dir = together((projected[:tok_count], projected[tok_count:]), "tensor")
    diff = outputs - targets.astype(jnp.float32)
    weighted = live_rows[:, None] * diff
    local_loss = jnp.sum(weighted * diff) * (1.0 / tensor_count)
    residual = weighted.astype(jnp.bfloat16)
    residual_dir = (live_rows[:, None] * out_dir).astype(jnp.bfloat16)
    back_prod = jnp.dot(
        jnp.concatenate([residual, residual_dir], axis=0),
        full_down,
        preferred_element_type=jnp.float32,
    )
    grad_h = back_prod[:tok_count]
    grad_dir = back_prod[tok_count:]
    chain_grad = (grad_dir * gelu_slope + grad_h * gelu_curve * tangent).astype(jnp.bfloat16)
    columns = tokens
    product = jnp.einsum("tr,tf->rf", columns, chain_grad, preferred_element_type=jnp.float32)
    sign_rows = all_signs
    hutch_terms = sign_rows.astype(jnp.float32) * product
    own_share = sum_in_two_steps(
        hutch_terms.reshape(own_rows * lax.axis_size(DP), ff_local // BLOCK, BLOCK).mean(axis=-1),
        (("dp_0", "dp_1", "dp_2"), "dp_3"),
        0,
    )
    loss_sum, total_count = (
        one_axis_at_a_time(local_loss, DP_TENSOR),
        one_axis_at_a_time(local_count, DP_TENSOR),
    )
    hess_diag = own_share / total_count
    second_moment = beta_two * moment + (1.0 - beta_two) * hess_diag * hess_diag
    mean_loss = loss_sum / (2.0 * total_count)
    return (hess_diag, second_moment, mean_loss)


def solution(mesh):
    torus = Mesh(
        mesh.devices.reshape(4, 4, 4, 2, mesh.shape["tensor"]),
        ("dp_0", "dp_1", "dp_2", "dp_3", "tensor"),
    )
    placed = (
        P(DP, None),
        P(DP, None),
        P(DP),
        P(DP, "tensor"),
        P(DP, "tensor"),
        P(),
        P("tensor"),
        P(DP, "tensor"),
    )
    return jax.shard_map(
        body,
        mesh=torus,
        in_specs=placed,
        out_specs=(P(DP, "tensor"), P(DP, "tensor"), P()),
        check_vma=False,
    )
```

profile of v0, /device:TPU:1, one launch (start us, length us, event | category | flops | bytes accessed | tf_op | source)
XLA Modules:
  0.0 491.9 jit_solution(3638978809061497128)
XLA Ops:
  9.4 15.8 %add_convert_fusion = bf16[1792,3584]{0,1:T(8,128)(2,1)} fusion(s32[3584]{0:T(1024)} %param.14, s32[1792]{0:T(1024)S(1)} %broadcast_multiply_fusion.1), kind=kLoop, calls=%fused_computation.13 | loop fusion | flops 109182976 | bytes 12866560 | tf_op jit(solution)/shard_map/convert_element_type | solution.py:65
  25.2 99.8 %all-gather.5.cloned.1.call-done = bf16[128,14,3584]{2,1,0:T(8,128)(2,1)} async-done(((bf16[1,14,3584]{2,1,0:T(8,128)(2,1)}), bf16[128,14,3584]{2,1,0:T(8,128)(2,1)}) %all-gather.5.cloned.1.call-update) | async-done | bytes 12845072 | tf_op jit(solution)/shard_map/all_gather | solution.py:92
  125.0 16.8 %reshape.48 = bf16[1792,3584]{1,0:T(8,128)(2,1)} reshape(bf16[128,14,3584]{2,1,0:T(8,128)(2,1)} %all-gather.5.cloned.1.call-done) | data formatting | bytes 25690112
  141.9 17.9 %copy.27 = bf16[1792,3584]{0,1:T(8,128)(2,1)} copy(bf16[1792,3584]{1,0:T(8,128)(2,1)} %reshape.48) | data formatting | bytes 25690112
  159.8 15.2 %fusion.10 = f32[128,7168]{1,0:T(8,128)} fusion(bf16[128,1792]{1,0:T(8,128)(2,1)S(1)} %copy-done, bf16[1792,3584]{0,1:T(8,128)(2,1)} %add_convert_fusion, bf16[1792,3584]{0,1:T(8,128)(2,1)} %copy.27), kind=kOutput, calls=%fused_computation.14 | convolution fusion | flops 3339714560 | bytes 29818880 | tf_op jit(solution)/shard_map/dot_general | solution.py:93
  175.0 3.3 multiply_convert_fusion.1
  178.3 57.5 %all-gather.7.cloned.1.call-done = bf16[128,14,3584]{2,1,0:T(8,128)(2,1)} async-done(((bf16[1,14,3584]{2,1,0:T(8,128)(2,1)}), bf16[128,14,3584]{2,1,0:T(8,128)(2,1)}) %all-gather.7.cloned.1.call-update) | async-done | bytes 12845072 | tf_op jit(solution)/shard_map/all_gather | solution.py:96
  235.8 16.8 %reshape.50 = bf16[1792,3584]{1,0:T(8,128)(2,1)} reshape(bf16[128,14,3584]{2,1,0:T(8,128)(2,1)} %all-gather.7.cloned.1.call-done) | data formatting | bytes 25690112
  252.6 7.0 %fusion.23 = f32[256,1792]{1,0:T(8,128)S(1)} fusion(bf16[1792,3584]{1,0:T(8,128)(2,1)} %reshape.50, bf16[128,3584]{1,0:T(8,128)(2,1)S(1)} %get-tuple-element.16, bf16[128,3584]{1,0:T(8,128)(2,1)S(1)} %get-tuple-element.15), kind=kOutput, calls=%fused_computation.29 | convolution fusion | flops 3292004352 | bytes 16515072 | tf_op jit(solution)/shard_map/tf,df->td/dot_general | solution.py:101
  260.1 3.3 broadcast_in_dim.2
  263.3 5.7 %all-to-all-start = ((f32[2,1,458752]{2,1,0:T(1,128)}), f32[2,1,458752]{2,1,0:T(1,128)}, u32[]{:S(2)}, u32[]{:S(2)}) async-start(f32[2,1,458752]{2,1,0:T(1,128)} %broadcast_in_dim.2), calls=%async_computation | async-start | bytes 7340032 | tf_op jit(solution)/shard_map/all_to_all | solution.py:17
  269.1 41.4 %all-to-all-done = f32[2,1,458752]{2,1,0:T(1,128)} async-done(((f32[2,1,458752]{2,1,0:T(1,128)}), f32[2,1,458752]{2,1,0:T(1,128)}, u32[]{:S(2)}, u32[]{:S(2)}) %all-to-all-start) | async-done | bytes 3670048 | tf_op jit(solution)/shard_map/all_to_all | solution.py:17
  310.5 18.1 %reduce_sum.54 = f32[458752]{0:T(1024)S(1)} reduce(f32[2,1,458752]{2,1,0:T(1,128)} %all-to-all-done, f32[]{:T(128)} %constant.20.clone.1), dimensions={0,1}, to_apply=%region_0.0 | reduce | flops 458752 | bytes 5505028 | tf_op jit(solution)/shard_map/reduce_sum | solution.py:22
  329.7 1.3 slice.49
  331.2 2.0 fusion.27
  333.1 6.7 %fusion.29 = f32[256,3584]{1,0:T(8,128)S(1)} fusion(bf16[1792,3584]{1,0:T(8,128)(2,1)} %reshape.50, bf16[128,1792]{1,0:T(8,128)(2,1)S(1)} %get-tuple-element.23, bf16[128,1792]{1,0:T(8,128)(2,1)S(1)} %get-tuple-element.22), kind=kOutput, calls=%fused_computation.41 | convolution fusion | flops 3290169344 | bytes 17432576 | tf_op jit(solution)/shard_map/dot_general | solution.py:108
  339.8 17.9 %bitcast_multiply_fusion = f32[1792,3584]{0,1:T(8,128)} fusion(bf16[128,1792]{1,0:T(8,128)(2,1)S(1)} %copy-done, s32[3584]{0:T(1024)S(1)} %copy-done.3, s32[1792]{0:T(1024)S(1)} %broadcast_multiply_fusion.1, f32[256,3584]{1,0:T(8,128)S(1)} %fusion.29, f32[128,7168]{1,0:T(8,128)S(1)} %copy-done.2), kind=kOutput, calls=%fused_computation.12 | convolution fusion | flops 1779957760 | bytes 33510400 | tf_op jit(solution)/shard_map/tr,tf->rf/dot_general | solution.py:117
  357.7 26.7 %reshape.46 = f32[1792,256,14]{0,2,1:T(8,128)} reshape(f32[1792,3584]{0,1:T(8,128)} %bitcast_multiply_fusion) | data formatting | bytes 51380224 | tf_op jit(solution)/shard_map/reshape | solution.py:121
  384.4 13.6 %reduce_sum.55 = f32[1792,256]{0,1:T(8,128)} reduce(f32[1792,256,14]{0,2,1:T(8,128)} %reshape.46, f32[]{:T(128)} %constant.20.clone.1), dimensions={2}, to_apply=%region_1.0 | reduce | flops 5963776 | bytes 27525124 | tf_op jit(solution)/shard_map/reduce_sum | solution.py:121
  398.0 1.7 broadcast_multiply_fusion
  399.7 1.7 copy.29
  401.4 1.6 div.19
  403.0 1.1 copy.30
  404.1 6.1 %all_to_all.16 = f32[2,64,14,256]{3,1,2,0:T(8,128)S(1)} all-to-all(f32[2,64,14,256]{3,1,2,0:T(8,128)S(1)} %copy.30), channel_id=1, replica_groups=mesh['dp_0'=4,'dp_1'=4,'dp_2'=4,'dp_3'=2,'tensor'=2] {'dp_3'}, dimensions={0} | all-to-all | bytes 3670016 | tf_op jit(solution)/shard_map/all_to_all | solution.py:41
  410.4 1.5 copy.31
  411.9 9.3 %all-to-all-start.2 = ((f32[64,14,256]{2,1,0:T(8,128)}), f32[64,14,256]{2,1,0:T(8,128)S(1)}, u32[]{:S(2)}, u32[]{:S(2)}) async-start(f32[64,14,256]{2,1,0:T(8,128)} %copy.31), calls=%async_computation.2 | async-start | bytes 2097152 | tf_op jit(solution)/shard_map/all_to_all | solution.py:48
  423.1 26.9 %all-reduce.2 = (f32[]{:T(128)}, f32[]{:T(128)}) all-reduce(f32[]{:T(128)S(6)} %mul.184, f32[]{:T(128)S(6)} %mul.191), channel_id=1, replica_groups=mesh['dp_0'=4,'dp_1'=4,'dp_2'=4,'dp_3'=2,'tensor'=2] {'dp_0'}, use_global_device_ids=true, to_apply=%region_5.0 | all-reduce | flops 2 | bytes 16 | tf_op jit(solution)/shard_map/psum | solution.py:53
  450.1 8.9 %all-reduce.1 = (f32[]{:T(128)}, f32[]{:T(128)}) all-reduce(f32[]{:T(128)} %get-tuple-element.7, f32[]{:T(128)} %get-tuple-element.8), channel_id=1, replica_groups=mesh['dp_0'=4,'dp_1'=4,'dp_2'=4,'dp_3'=2,'tensor'=2] {'dp_1'}, use_global_device_ids=true, to_apply=%region_6.0 | all-reduce | flops 2 | bytes 16 | tf_op jit(solution)/shard_map/psum | solution.py:53
  459.0 8.8 %all-reduce = (f32[]{:T(128)}, f32[]{:T(128)}) all-reduce(f32[]{:T(128)} %get-tuple-element.5, f32[]{:T(128)} %get-tuple-element.6), channel_id=1, replica_groups=mesh['dp_0'=4,'dp_1'=4,'dp_2'=4,'dp_3'=2,'tensor'=2] {'dp_2'}, use_global_device_ids=true, to_apply=%region_7.0 | all-reduce | flops 2 | bytes 16 | tf_op jit(solution)/shard_map/psum | solution.py:53
  467.8 8.8 %all-reduce.4 = (f32[]{:T(128)}, f32[]{:T(128)}) all-reduce(f32[]{:T(128)} %get-tuple-element.3, f32[]{:T(128)} %get-tuple-element.4), channel_id=1, replica_groups=mesh['dp_0'=4,'dp_1'=4,'dp_2'=4,'dp_3'=2,'tensor'=2] {'dp_3'}, use_global_device_ids=true, to_apply=%region_8.0 | all-reduce | flops 2 | bytes 16 | tf_op jit(solution)/shard_map/psum | solution.py:53
  476.5 4.6 all-reduce.3
  482.7 1.3 fusion.39
  (28 shorter events, 4.7 us)
Async XLA Ops:
  7.2 152.6 %copy-start = (bf16[128,1792]{1,0:T(8,128)(2,1)S(1)}, bf16[128,1792]{1,0:T(8,128)(2,1)}, u32[]{:S(2)}) copy-start(bf16[128,1792]{1,0:T(8,128)(2,1)} %param.8) | copy-start | bytes 1376260
  7.2 117.9 %all-gather.5.cloned.1.call-start = ((), (), s32[]{:S(2)}) async-start(), calls=%async_computation.3 | async-start | bytes 14794752 | tf_op jit(solution)/shard_map/all_gather | solution.py:92
  7.9 227.9 %all-gather.7.cloned.1.call-start = ((), (), s32[]{:S(2)}) async-start(), calls=%async_computation.4 | async-start | bytes 14794752 | tf_op jit(solution)/shard_map/all_gather | solution.py:96
  263.3 5.7 %copy-start.5 = (s32[128]{0:T(128)S(1)}, s32[128]{0:T(128)}, u32[]{:S(2)}) copy-start(s32[128]{0:T(128)} %param.10) | copy-start | bytes 1540
  263.3 47.2 %all-to-all-start = ((f32[2,1,458752]{2,1,0:T(1,128)}), f32[2,1,458752]{2,1,0:T(1,128)}, u32[]{:S(2)}, u32[]{:S(2)}) async-start(f32[2,1,458752]{2,1,0:T(1,128)} %broadcast_in_dim.2), calls=%async_computation | async-start | bytes 7340032 | tf_op jit(solution)/shard_map/all_to_all | solution.py:17
  333.1 6.7 %copy-start.2 = (f32[128,7168]{1,0:T(8,128)S(1)}, f32[128,7168]{1,0:T(8,128)}, u32[]{:S(2)}) copy-start(f32[128,7168]{1,0:T(8,128)} %fusion.10) | copy-start | bytes 11010052
  333.1 6.7 %copy-start.3 = (s32[3584]{0:T(1024)S(1)}, s32[3584]{0:T(1024)}, u32[]{:S(2)}) copy-start(s32[3584]{0:T(1024)} %param.14) | copy-start | bytes 43012
  404.1 79.9 %copy-start.1 = (bf16[128,1792]{1,0:T(8,128)(2,1)S(1)}, bf16[128,1792]{1,0:T(8,128)(2,1)}, u32[]{:S(2)}) copy-start(bf16[128,1792]{1,0:T(8,128)(2,1)} %param.8) | copy-start | bytes 1376260
  410.2 72.5 %copy-start.4 = (f32[14,256]{1,0:T(8,128)S(1)}, f32[14,256]{1,0:T(8,128)}, u32[]{:S(2)}) copy-start(f32[14,256]{1,0:T(8,128)} %param.15) | copy-start | bytes 43012
  411.9 70.6 %all-to-all-start.2 = ((f32[64,14,256]{2,1,0:T(8,128)}), f32[64,14,256]{2,1,0:T(8,128)S(1)}, u32[]{:S(2)}, u32[]{:S(2)}) async-start(f32[64,14,256]{2,1,0:T(8,128)} %copy.31), calls=%async_computation.2 | async-start | bytes 2097152 | tf_op jit(solution)/shard_map/all_to_all | solution.py:48
Sparse Core Ops, SparseCore 0:
  11.4 113.6 all-gather.4
  128.5 107.3 all-gather.6
where the time goes:
time: 495 us; the launch traced here: 492 us
  waiting for transfers between devices  200 us (40%)
  local copies, waits for them, and re-layouts  90.2 us (18%)
  blocking collectives  64.2 us (13%)
  other arithmetic  57.6 us (12%)
  matrix products  46.8 us (9%)
  between operations  18 us (4%)
  starting transfers between devices  15.1 us (3%)
    all_gather x1, waiting for transfers between devices, body(): lax.all_gather(up_weight, DP, axis=0, tiled=True)  99.8 us
    psum x5, blocking collectives, one_axis_at_a_time(): shard = lax.psum(shard, axis)  58.1 us
    all_gather x1, waiting for transfers between devices, body(): full_down = lax.all_gather(down_weight, DP, axis=0, tiled=True)  57.5 us
    unnamed x15, local copies, waits for them, and re-layouts  51.6 us
    all_to_all x1, waiting for transfers between devices, sent_to_all(): return lax.all_to_all(copies, axis, split_axis=0, concat_axis=0, tiled=True)  41.4 us
    reshape x1, local copies, waits for them, and re-layouts, body(): hutch_terms.reshape(own_rows * lax.axis_size(DP), ff_local // BLOCK, BLOCK)  26.7 us
    reduce_sum x1, other arithmetic, over_copies(): return jnp.sum(everything, axis=0)  18.1 us
    dot_general x1, matrix products, body(): jnp.einsum('tr,tf->rf', columns, chain_grad, preferred_element_type=jnp.f...  17.9 us
  transfers between devices with their start and end apart: 4, of which 3 were waited for; matrix products, arithmetic and copies ran while one was open for 14% of the time, Pallas kernels for 0%

commit v1 on v0

--- a/solution.py
+++ b/solution.py
@@ -3,6 +3,7 @@
 from jax import lax
 from jax.sharding import Mesh
 from jax.sharding import PartitionSpec as P
+from jax.lax import all_gather
 
 BLOCK = 14
 DP = ("dp_0", "dp_1", "dp_2", "dp_3")
@@ -50,7 +51,12 @@
 
 def one_axis_at_a_time(shard, axes):
     for axis in axes:
-        shard = lax.psum(shard, axis)
+
+        def try_all_the_forms(raw):
+            m_next = jnp.sum(all_gather(raw, axis_name=axis), axis=0)
+            return m_next
+
+        shard = try_all_the_forms(shard)
     return shard
 
 

time: 495 us -> 511 us (1.032)
  local copies, waits for them, and re-layouts: 90.2 us -> 106 us
  other arithmetic: 57.6 us -> 63.7 us
  blocking collectives: 64.2 us -> 58.1 us
    psum x5 -> x0, blocking collectives: 58.1 us -> none  [one_axis_at_a_time(): shard = lax.psum(shard, axis)]
    unnamed x0 -> x5, blocking collectives: none -> 52 us
    unnamed x15 -> x50, local copies, waits for them, and re-layouts: 51.6 us -> 67.5 us
    reduce_sum x0 -> x10, other arithmetic: none -> 6.09 us  [try_all_the_forms(): m_next = jnp.sum(all_gather(raw, axis_name=axis), axis=0)]
  transfers between devices with their start and end apart: 4 -> 4, of which waited for: 3 -> 3; matrix products, arithmetic and copies ran while one was open for 14% -> 18% of each run, Pallas kernels for 0% -> 0%
where the time goes in v1:
time: 511 us; the launch traced here: 508 us
  waiting for transfers between devices  200 us (39%)
  local copies, waits for them, and re-layouts  106 us (21%)
  other arithmetic  63.7 us (12%)
  blocking collectives  58.1 us (11%)
  matrix products  46.8 us (9%)
  between operations  18.1 us (4%)
  starting transfers between devices  15.1 us (3%)
    all_gather x1, waiting for transfers between devices, body(): lax.all_gather(up_weight, DP, axis=0, tiled=True)  99.8 us
    unnamed x50, local copies, waits for them, and re-layouts  67.5 us
    all_gather x1, waiting for transfers between devices, body(): full_down = lax.all_gather(down_weight, DP, axis=0, tiled=True)  57.5 us
    unnamed x5, blocking collectives  52 us
    all_to_all x1, waiting for transfers between devices, sent_to_all(): return lax.all_to_all(copies, axis, split_axis=0, concat_axis=0, tiled=True)  41.4 us
    reshape x1, local copies, waits for them, and re-layouts, body(): hutch_terms.reshape(own_rows * lax.axis_size(DP), ff_local // BLOCK, BLOCK)  26.7 us
    reduce_sum x1, other arithmetic, over_copies(): return jnp.sum(everything, axis=0)  18.1 us
    dot_general x1, matrix products, body(): jnp.einsum('tr,tf->rf', columns, chain_grad, preferred_element_type=jnp.f...  17.9 us
  transfers between devices with their start and end apart: 4, of which 3 were waited for; matrix products, arithmetic and copies ran while one was open for 18% of the time, Pallas kernels for 0%

profile of v1, /device:TPU:1, one launch (start us, length us, event | category | flops | bytes accessed | tf_op | source)
XLA Modules:
  0.0 507.9 jit_solution(455806636902004560)
XLA Ops:
  9.4 15.8 %add_convert_fusion = bf16[1792,3584]{0,1:T(8,128)(2,1)} fusion(s32[3584]{0:T(1024)} %param.14, s32[1792]{0:T(1024)S(1)} %broadcast_multiply_fusion.1), kind=kLoop, calls=%fused_computation.13 | loop fusion | flops 109182976 | bytes 12866560 | tf_op jit(solution)/shard_map/convert_element_type | solution.py:71
  25.2 99.8 %all-gather.5.cloned.1.call-done = bf16[128,14,3584]{2,1,0:T(8,128)(2,1)} async-done(((bf16[1,14,3584]{2,1,0:T(8,128)(2,1)}), bf16[128,14,3584]{2,1,0:T(8,128)(2,1)}) %all-gather.5.cloned.1.call-update) | async-done | bytes 12845072 | tf_op jit(solution)/shard_map/all_gather | solution.py:98
  125.0 16.8 %reshape.78 = bf16[1792,3584]{1,0:T(8,128)(2,1)} reshape(bf16[128,14,3584]{2,1,0:T(8,128)(2,1)} %all-gather.5.cloned.1.call-done) | data formatting | bytes 25690112
  141.9 17.9 %copy.27 = bf16[1792,3584]{0,1:T(8,128)(2,1)} copy(bf16[1792,3584]{1,0:T(8,128)(2,1)} %reshape.78) | data formatting | bytes 25690112
  159.8 15.2 %fusion.10 = f32[128,7168]{1,0:T(8,128)} fusion(bf16[128,1792]{1,0:T(8,128)(2,1)S(1)} %copy-done, bf16[1792,3584]{0,1:T(8,128)(2,1)} %add_convert_fusion, bf16[1792,3584]{0,1:T(8,128)(2,1)} %copy.27), kind=kOutput, calls=%fused_computation.14 | convolution fusion | flops 3339714560 | bytes 29818880 | tf_op jit(solution)/shard_map/dot_general | solution.py:99
  175.0 3.3 multiply_convert_fusion.1
  178.3 57.5 %all-gather.7.cloned.1.call-done = bf16[128,14,3584]{2,1,0:T(8,128)(2,1)} async-done(((bf16[1,14,3584]{2,1,0:T(8,128)(2,1)}), bf16[128,14,3584]{2,1,0:T(8,128)(2,1)}) %all-gather.7.cloned.1.call-update) | async-done | bytes 12845072 | tf_op jit(solution)/shard_map/all_gather | solution.py:102
  235.8 16.8 %reshape.80 = bf16[1792,3584]{1,0:T(8,128)(2,1)} reshape(bf16[128,14,3584]{2,1,0:T(8,128)(2,1)} %all-gather.7.cloned.1.call-done) | data formatting | bytes 25690112
  252.6 7.0 %fusion.23 = f32[256,1792]{1,0:T(8,128)S(1)} fusion(bf16[1792,3584]{1,0:T(8,128)(2,1)} %reshape.80, bf16[128,3584]{1,0:T(8,128)(2,1)S(1)} %get-tuple-element.16, bf16[128,3584]{1,0:T(8,128)(2,1)S(1)} %get-tuple-element.15), kind=kOutput, calls=%fused_computation.29 | convolution fusion | flops 3292004352 | bytes 16515072 | tf_op jit(solution)/shard_map/tf,df->td/dot_general | solution.py:107
  260.1 3.3 broadcast_in_dim.2
  263.3 5.7 %all-to-all-start = ((f32[2,1,458752]{2,1,0:T(1,128)}), f32[2,1,458752]{2,1,0:T(1,128)}, u32[]{:S(2)}, u32[]{:S(2)}) async-start(f32[2,1,458752]{2,1,0:T(1,128)} %broadcast_in_dim.2), calls=%async_computation | async-start | bytes 7340032 | tf_op jit(solution)/shard_map/all_to_all | solution.py:18
  269.1 41.4 %all-to-all-done = f32[2,1,458752]{2,1,0:T(1,128)} async-done(((f32[2,1,458752]{2,1,0:T(1,128)}), f32[2,1,458752]{2,1,0:T(1,128)}, u32[]{:S(2)}, u32[]{:S(2)}) %all-to-all-start) | async-done | bytes 3670048 | tf_op jit(solution)/shard_map/all_to_all | solution.py:18
  310.5 18.1 %reduce_sum.144 = f32[458752]{0:T(1024)S(1)} reduce(f32[2,1,458752]{2,1,0:T(1,128)} %all-to-all-done, f32[]{:T(128)} %constant.20.clone.1), dimensions={0,1}, to_apply=%region_0.0 | reduce | flops 458752 | bytes 5505028 | tf_op jit(solution)/shard_map/reduce_sum | solution.py:23
  331.2 2.0 fusion.27
  333.1 6.7 %fusion.29 = f32[256,3584]{1,0:T(8,128)S(1)} fusion(bf16[1792,3584]{1,0:T(8,128)(2,1)} %reshape.80, bf16[128,1792]{1,0:T(8,128)(2,1)S(1)} %get-tuple-element.23, bf16[128,1792]{1,0:T(8,128)(2,1)S(1)} %get-tuple-element.22), kind=kOutput, calls=%fused_computation.41 | convolution fusion | flops 3290169344 | bytes 17432576 | tf_op jit(solution)/shard_map/dot_general | solution.py:114
  339.8 17.9 %bitcast_multiply_fusion = f32[1792,3584]{0,1:T(8,128)} fusion(bf16[128,1792]{1,0:T(8,128)(2,1)S(1)} %copy-done, s32[3584]{0:T(1024)S(1)} %copy-done.3, s32[1792]{0:T(1024)S(1)} %broadcast_multiply_fusion.1, f32[256,3584]{1,0:T(8,128)S(1)} %fusion.29, f32[128,7168]{1,0:T(8,128)S(1)} %copy-done.2), kind=kOutput, calls=%fused_computation.12 | convolution fusion | flops 1779957760 | bytes 33510400 | tf_op jit(solution)/shard_map/tr,tf->rf/dot_general | solution.py:123
  357.7 26.7 %reshape.46 = f32[1792,256,14]{0,2,1:T(8,128)} reshape(f32[1792,3584]{0,1:T(8,128)} %bitcast_multiply_fusion) | data formatting | bytes 51380224 | tf_op jit(solution)/shard_map/reshape | solution.py:127
  384.4 13.6 %reduce_sum.145 = f32[1792,256]{0,1:T(8,128)} reduce(f32[1792,256,14]{0,2,1:T(8,128)} %reshape.46, f32[]{:T(128)} %constant.20.clone.1), dimensions={2}, to_apply=%region_1.0 | reduce | flops 5963776 | bytes 27525124 | tf_op jit(solution)/shard_map/reduce_sum | solution.py:127
  398.0 1.7 broadcast_multiply_fusion
  399.7 1.7 copy.29
  401.4 1.6 div.19
  404.1 6.1 %all_to_all.16 = f32[2,64,14,256]{3,1,2,0:T(8,128)S(1)} all-to-all(f32[2,64,14,256]{3,1,2,0:T(8,128)S(1)} %copy.30), channel_id=1, replica_groups=mesh['dp_0'=4,'dp_1'=4,'dp_2'=4,'dp_3'=2,'tensor'=2] {'dp_3'}, dimensions={0} | all-to-all | bytes 3670016 | tf_op jit(solution)/shard_map/all_to_all | solution.py:42
  410.4 1.5 copy.31
  412.0 9.3 %all-to-all-start.2 = ((f32[64,14,256]{2,1,0:T(8,128)}), f32[64,14,256]{2,1,0:T(8,128)S(1)}, u32[]{:S(2)}, u32[]{:S(2)}) async-start(f32[64,14,256]{2,1,0:T(8,128)} %copy.31), calls=%async_computation.2 | async-start | bytes 2097152 | tf_op jit(solution)/shard_map/all_to_all | solution.py:49
  426.1 23.5 %all-reduce.12 = (f32[4]{0:T(128)S(1)}, f32[4]{0:T(128)S(1)}) all-reduce(f32[4]{0:T(128)S(1)} %dynamic-update-slice, f32[4]{0:T(128)S(1)} %dynamic-update-slice.5), channel_id=1, replica_groups=mesh['dp_0'=4,'dp_1'=4,'dp_2'=4,'dp_3'=2,'tensor'=2] {'dp_0'}, use_global_device_ids=true, to_apply=%add | all-reduce | flops 8 | bytes 64
  452.2 1.4 dynamic-update-slice.6
  454.2 8.3 %all-reduce.11 = (f32[4]{0:T(128)S(1)}, f32[4]{0:T(128)S(1)}) all-reduce(f32[4]{0:T(128)S(1)} %dynamic-update-slice.1, f32[4]{0:T(128)S(1)} %dynamic-update-slice.6), channel_id=1, replica_groups=mesh['dp_0'=4,'dp_1'=4,'dp_2'=4,'dp_3'=2,'tensor'=2] {'dp_1'}, use_global_device_ids=true, to_apply=%add.1 | all-reduce | flops 8 | bytes 64
  467.1 8.1 %all-reduce.10 = (f32[4]{0:T(128)S(1)}, f32[4]{0:T(128)S(1)}) all-reduce(f32[4]{0:T(128)S(1)} %dynamic-update-slice.2, f32[4]{0:T(128)S(1)} %dynamic-update-slice.7), channel_id=1, replica_groups=mesh['dp_0'=4,'dp_1'=4,'dp_2'=4,'dp_3'=2,'tensor'=2] {'dp_2'}, use_global_device_ids=true, to_apply=%add.2 | all-reduce | flops 8 | bytes 64
  477.8 1.4 dynamic-update-slice.8
  479.8 8.1 %all-reduce.14 = (f32[2]{0:T(128)S(1)}, f32[2]{0:T(128)S(1)}) all-reduce(f32[2]{0:T(128)S(1)} %dynamic-update-slice.3, f32[2]{0:T(128)S(1)} %dynamic-update-slice.8), channel_id=1, replica_groups=mesh['dp_0'=4,'dp_1'=4,'dp_2'=4,'dp_3'=2,'tensor'=2] {'dp_3'}, use_global_device_ids=true, to_apply=%add.3 | all-reduce | flops 4 | bytes 32
  490.5 1.4 dynamic-update-slice.9
  491.9 3.9 all-reduce.13
  (73 shorter events, 26.2 us)
Async XLA Ops:
  7.2 152.6 %copy-start = (bf16[128,1792]{1,0:T(8,128)(2,1)S(1)}, bf16[128,1792]{1,0:T(8,128)(2,1)}, u32[]{:S(2)}) copy-start(bf16[128,1792]{1,0:T(8,128)(2,1)} %param.8) | copy-start | bytes 1376260
  7.2 117.9 %all-gather.5.cloned.1.call-start = ((), (), s32[]{:S(2)}) async-start(), calls=%async_computation.3 | async-start | bytes 14794752 | tf_op jit(solution)/shard_map/all_gather | solution.py:98
  7.9 227.9 %all-gather.7.cloned.1.call-start = ((), (), s32[]{:S(2)}) async-start(), calls=%async_computation.4 | async-start | bytes 14794752 | tf_op jit(solution)/shard_map/all_gather | solution.py:102
  263.3 5.7 %copy-start.5 = (s32[128]{0:T(128)S(1)}, s32[128]{0:T(128)}, u32[]{:S(2)}) copy-start(s32[128]{0:T(128)} %param.10) | copy-start | bytes 1540
  263.3 47.2 %all-to-all-start = ((f32[2,1,458752]{2,1,0:T(1,128)}), f32[2,1,458752]{2,1,0:T(1,128)}, u32[]{:S(2)}, u32[]{:S(2)}) async-start(f32[2,1,458752]{2,1,0:T(1,128)} %broadcast_in_dim.2), calls=%async_computation | async-start | bytes 7340032 | tf_op jit(solution)/shard_map/all_to_all | solution.py:18
  333.1 6.7 %copy-start.2 = (f32[128,7168]{1,0:T(8,128)S(1)}, f32[128,7168]{1,0:T(8,128)}, u32[]{:S(2)}) copy-start(f32[128,7168]{1,0:T(8,128)} %fusion.10) | copy-start | bytes 11010052
  333.1 6.7 %copy-start.3 = (s32[3584]{0:T(1024)S(1)}, s32[3584]{0:T(1024)}, u32[]{:S(2)}) copy-start(s32[3584]{0:T(1024)} %param.14) | copy-start | bytes 43012
  404.1 95.9 %copy-start.1 = (bf16[128,1792]{1,0:T(8,128)(2,1)S(1)}, bf16[128,1792]{1,0:T(8,128)(2,1)}, u32[]{:S(2)}) copy-start(bf16[128,1792]{1,0:T(8,128)(2,1)} %param.8) | copy-start | bytes 1376260
  410.2 12.3 %copy-start.10 = (u32[256]{0:T(256)S(1)}, u32[256]{0:T(256)}, u32[]{:S(2)}) copy-start(u32[256]{0:T(256)} %constant.55) | copy-start | bytes 3076
  410.2 15.3 %copy-start.9 = (u32[256]{0:T(256)S(1)}, u32[256]{0:T(256)}, u32[]{:S(2)}) copy-start(u32[256]{0:T(256)} %constant.60) | copy-start | bytes 3076
  410.2 43.4 %copy-start.8 = (u32[256]{0:T(256)S(1)}, u32[256]{0:T(256)}, u32[]{:S(2)}) copy-start(u32[256]{0:T(256)} %constant.65) | copy-start | bytes 3076
  410.2 56.3 %copy-start.7 = (u32[256]{0:T(256)S(1)}, u32[256]{0:T(256)}, u32[]{:S(2)}) copy-start(u32[256]{0:T(256)} %constant.70) | copy-start | bytes 3076
  410.2 69.0 %copy-start.6 = (u32[256]{0:T(256)S(1)}, u32[256]{0:T(256)}, u32[]{:S(2)}) copy-start(u32[256]{0:T(256)} %constant.75) | copy-start | bytes 3076
  410.2 88.4 %copy-start.4 = (f32[14,256]{1,0:T(8,128)S(1)}, f32[14,256]{1,0:T(8,128)}, u32[]{:S(2)}) copy-start(f32[14,256]{1,0:T(8,128)} %param.15) | copy-start | bytes 43012
  412.0 86.6 %all-to-all-start.2 = ((f32[64,14,256]{2,1,0:T(8,128)}), f32[64,14,256]{2,1,0:T(8,128)S(1)}, u32[]{:S(2)}, u32[]{:S(2)}) async-start(f32[64,14,256]{2,1,0:T(8,128)} %copy.31), calls=%async_computation.2 | async-start | bytes 2097152 | tf_op jit(solution)/shard_map/all_to_all | solution.py:49
Sparse Core Ops, SparseCore 0:
  11.4 113.6 all-gather.4
  128.5 107.3 all-gather.6
